TPU v7x, 32 devices: a whole 2x2x4 slice. The times are simulated.
32 devices in a mesh: section: 4 (over x, core), ep: 8 (over z, y).
Axes of the slice: x: 2, y: 2, z: 4, core: 2. Of those that a mesh axis runs over, the one named last changes fastest.
Arguments:
- output_grad: bfloat16 [4, 2048, 1024], P('section', 'ep'), may hold values from -6 to 6
- layer_input: bfloat16 [4, 2048, 1024], P('section', 'ep'), may hold values from -6 to 6
- expert_ids: int32 [4, 2048, 8], P('section', 'ep'), may hold values from 0 to 31, all different within a row; in each aligned block of 256 rows (0 to 255, 256 to 511, ..., all dimensions but the last counted through in order) at most 80 rows name the same one
- route_probs: bfloat16 [4, 2048, 8], P('section', 'ep'), may hold values from 0.049804688 to 0.44921875
- gate_weight: bfloat16 [4, 32, 1024, 384], P('section', 'ep'), may hold values from -0.1875 to 0.1875
- up_weight: bfloat16 [4, 32, 1024, 384], P('section', 'ep'), may hold values from -0.1875 to 0.1875
- down_weight: bfloat16 [4, 32, 384, 1024], P('section', 'ep'), may hold values from -0.3125 to 0.3125
- saved_inputs: bfloat16 [4, 32, 640, 1024], P('section', 'ep'), may hold values from -6 to 6
- saved_gate_grad: bfloat16 [4, 32, 640, 384], P('section', 'ep'), may hold values from -0.5 to 0.5
- saved_up_grad: bfloat16 [4, 32, 640, 384], P('section', 'ep'), may hold values from -0.5 to 0.5
- saved_counts: int32 [4, 32, 8], P('section', 'ep'), may hold values from 0 to 80, as said below
Outputs:
- upstream_grad: bfloat16 [4, 2048, 1024], P('section', 'ep')
- prob_grad: bfloat16 [4, 2048, 8], P('section', 'ep')
- gate_weight_grad: bfloat16 [4, 32, 1024, 384], P('section', 'ep')
- up_weight_grad: bfloat16 [4, 32, 1024, 384], P('section', 'ep')
Inputs may be any that keep to these rules, and one draw needn't show every extreme that they name: `expert_ids`: each token names 8 different experts. Among the tokens of one device (aligned blocks of 256 tokens of a section) no expert is named more than 80 times, a bound that some block reaches. `saved_counts`: rows of a block at or beyond its count are padding; some block is full in every draw.
All inputs are finite; a program needn't handle non-finite values.
Results may differ from a plain program's by a relative error of at most 0.008.
Values may be sent and summed in bfloat16 or wider, within the bound.
A program may use at most 128 MiB of HBM per device.

v0:
```python
import functools

import jax
import jax.numpy as jnp
from jax import lax
from jax.experimental import pallas as pl
from jax.experimental.pallas import tpu as pltpu
from jax.sharding import PartitionSpec as P

F32 = jnp.float32
BF16 = jnp.bfloat16
MESH = pl.DeviceIdType.MESH
VMEM = pl.BlockSpec(memory_space=pltpu.VMEM)
ANY = pl.BlockSpec(memory_space=pl.ANY)


class Copies:
    def __init__(self, send, recv):
        self.send, self.recv, self.used, self.items = send, recv, 0, []

    def start(self, src, dst, target, when=None):
        at = self.used
        self.used += 1
        copy = pltpu.make_async_remote_copy(
            src_ref=src,
            dst_ref=dst,
            send_sem=self.send.at[at],
            recv_sem=self.recv.at[at],
            device_id={"ep": target},
            device_id_type=MESH,
        )
        self.items.append((copy, when))
        guarded(when, copy.start)
        return copy

    def finish(self):
        for copy, when in self.items:
            guarded(when, copy.wait_send)


def guarded(when, act):
    if when is None:
        act()
    else:
        pl.when(when)(act)


def place_of(count):
    me = lax.axis_index("ep")
    outer, inner = me // 2, me % 2
    line = count // 2
    up = ((outer + 1) % line) * 2 + inner
    down = ((outer + line - 1) % line) * 2 + inner
    return me, outer, inner, line, (up, down), outer * 2 + 1 - inner


def gather_copies(count):
    line = count // 2
    return 12 * (line - 1) + 3 + (count - 1)


def weight_tile(live, held, saved, outs, expert):
    mask = live[expert][:, :1]
    grads = [ref[expert] * mask for ref in saved]
    tile = 256

    def body(at, carry):
        columns = pl.ds(pl.multiple_of(at * tile, tile), tile)
        rows = held[expert, :, columns]
        for grad, out in zip(grads, outs):
            out[expert, columns, :] = lax.dot_general(
                rows, grad, (((0,), (0,)), ((), ())), preferred_element_type=F32
            ).astype(BF16)
        return carry

    lax.fori_loop(0, held.shape[2] // tile, body, 0)


def gather_kernel(
    count, g, x, s, live, held_in, gate_in, up_in, g_all, x_all, s_all, gate_out, up_out, held,
    gate_held, up_held, local, send, recv,
):
    me, outer, inner, line, sides, partner = place_of(count)
    width = g.shape[1]
    cut = max(width * 3 // 1024, 1) * 128
    copies = Copies(send, recv)
    own = [
        pltpu.make_async_copy(g, g_all.at[me], local.at[0]),
        pltpu.make_async_copy(x, x_all.at[me], local.at[1]),
        pltpu.make_async_copy(s, s_all.at[me], local.at[2]),
    ]
    loads = [
        pltpu.make_async_copy(src, dst, local.at[3 + at])
        for at, (src, dst) in enumerate(((held_in, held), (gate_in, gate_held), (up_in, up_held)))
    ]
    for copy in own + loads:
        copy.start()
    barrier = pltpu.get_barrier_semaphore()
    for away in range(1, count):
        pl.semaphore_signal(
            barrier, inc=1, device_id={"ep": (me + away) % count}, device_id_type=MESH
        )
    pl.semaphore_wait(barrier, count - 1)
    everything, few, many = pl.ds(0, width), pl.ds(0, cut), pl.ds(cut, width - cut)

    def block(step, side):
        return (outer + (-step if side == 0 else step) + 2 * line) % line

    def arrives(step, side):
        return outer >= step + 1 if side == 0 else outer + step + 1 <= line - 1

    def leaves(step, side):
        if side == 0:
            return jnp.logical_and(outer >= step, outer < line - 1)
        return jnp.logical_and(outer + step <= line - 1, outer > 0)

    def hop(ref, all_ref, columns, step, side, row):
        dst = all_ref.at[block(step, side) * 2 + row, :, columns]
        source = dst if ref is None else ref.at[:, columns]
        return copies.start(source, dst, sides[side], leaves(step, side))

    def take(copy, step, side):
        guarded(arrives(step, side), copy.wait_recv)

    side_list = (0, 1)
    other = 1 - inner
    pieces = ((x, x_all, everything), (g, g_all, many))
    now = {}
    g_across = copies.start(g.at[:, few], g_all.at[me, :, few], partner)
    for at, (ref, all_ref, columns) in enumerate(pieces):
        for side in side_list:
            now[at, side] = hop(ref, all_ref, columns, 0, side, inner)
    for side in side_list:
        now[2, side] = hop(g, g_all, few, 0, side, inner)
    late = [
        (copies.start(x, x_all.at[me], partner), None),
        (copies.start(g.at[:, many], g_all.at[me, :, many], partner), None),
    ]
    for away in range(1, count):
        late.append((copies.start(s, s_all.at[me], (me + away) % count), None))
    experts = list(range(held.shape[0]))
    for copy in loads:
        copy.wait()

    def work():
        if experts:
            weight_tile(live, held, (gate_held, up_held), (gate_out, up_out), experts.pop(0))

    work()
    g_across.wait_recv()
    for side in side_list:
        now[3, side] = hop(None, g_all, few, 0, side, other)
    for step in range(line - 1):
        more = step < line - 2
        for at in range(4):
            row = other if at == 3 else inner
            all_ref, columns = pieces[at][1:] if at < 2 else (g_all, few)
            for side in side_list:
                take(now[at, side], step, side)
                if more:
                    now[at, side] = hop(None, all_ref, columns, step + 1, side, row)
                if at < 2:
                    got = all_ref.at[block(step + 1, side) * 2 + inner, :, columns]
                    has = arrives(step, side)
                    late.append((copies.start(got, got, partner, has), has))
            if at % 2 == 1:
                work()
    while experts:
        work()
    for copy, when in late:
        guarded(when, copy.wait_recv)
    copies.finish()
    for copy in own:
        copy.wait()


def gather_tokens(count, g, x, s, live, held, gate, up):
    pairs = gather_copies(count)
    grads = jax.ShapeDtypeStruct((held.shape[0], held.shape[2], gate.shape[2]), BF16)
    return pl.pallas_call(
        functools.partial(gather_kernel, count),
        out_shape=[jax.ShapeDtypeStruct((count,) + a.shape, a.dtype) for a in (g, x, s)]
        + [grads, grads],
        in_specs=[VMEM] * 4 + [ANY] * 3,
        out_specs=[ANY] * 3 + [VMEM] * 2,
        scratch_shapes=[
            pltpu.VMEM(held.shape, BF16),
            pltpu.VMEM(gate.shape, BF16),
            pltpu.VMEM(up.shape, BF16),
            pltpu.SemaphoreType.DMA((6,)),
            pltpu.SemaphoreType.DMA((pairs,)),
            pltpu.SemaphoreType.DMA((pairs,)),
        ],
        compiler_params=pltpu.CompilerParams(
            collective_id=0, has_side_effects=True, vmem_limit_bytes=48 * 1024 * 1024
        ),
    )(g, x, s, live, held, gate, up)


def scatter_copies(count):
    line = count // 2
    return line + 1 + (count - 1)


def add(a, b):
    return (a.astype(F32) + b.astype(F32)).astype(BF16)


def scatter_kernel(
    count, sections, part, prob, out, prob_out, a_sum, a_side, a_take, b_sum, b_side, land_a,
    land_b, send, recv, line_send, line_recv, shift_send, shift_recv,
):
    me, outer, inner, line, sides, partner = place_of(count)
    section = lax.axis_index("section")
    cut = a_sum.shape[3]
    copies = Copies(send, recv)
    barrier = pltpu.get_barrier_semaphore()
    for away in range(1, count):
        pl.semaphore_signal(
            barrier, inc=1, device_id={"ep": (me + away) % count}, device_id_type=MESH
        )
    for away in (1, sections - 1):
        pl.semaphore_signal(
            barrier, inc=1, device_id={"section": (section + away) % sections}, device_id_type=MESH
        )
    pl.semaphore_wait(barrier, count + 1)
    other = 1 - inner
    low, high = pl.ds(0, cut), pl.ds(cut, part.shape[2] - cut)

    def goal(at):
        mixed = line - 1 - at // 2 if at % 2 == 0 else at // 2
        return jnp.where(outer == 0, line - 1 - at, jnp.where(outer == line - 1, at, mixed))

    across = [
        copies.start(part.at[goal(at) * 2 + other, :, high], b_sum.at[goal(at)], partner)
        for at in range(line)
    ]
    tiny = [
        copies.start(prob.at[(me + away) % count], prob_out.at[me], (me + away) % count)
        for away in range(1, count)
    ]
    prob_out[me] = prob[me]

    def line_copy(kind, source, side_ref, side, place):
        return pltpu.make_async_remote_copy(
            src_ref=source.at[place],
            dst_ref=side_ref.at[side, place],
            send_sem=line_send.at[kind, side, place],
            recv_sem=line_recv.at[kind, side, place],
            device_id={"ep": sides[side]},
            device_id_type=MESH,
        )

    def collect(kind, total, side_ref, side, place):
        line_copy(kind, total, side_ref, side, place).wait_recv()
        total[place] = add(total[place], side_ref[side, place])

    def advance(kind, total, side_ref, place):
        @pl.when(jnp.logical_and(place >= outer, outer > 0))
        def _():
            collect(kind, total, side_ref, 0, place)

        @pl.when(jnp.logical_and(place <= outer, outer < line - 1))
        def _():
            collect(kind, total, side_ref, 1, place)

        @pl.when(place > outer)
        def _():
            line_copy(kind, total, side_ref, 0, place).start()

        @pl.when(place < outer)
        def _():
            line_copy(kind, total, side_ref, 1, place).start()

    for at in range(line):
        place = goal(at)
        for kind, row in ((0, other), (1, inner)):
            a_sum[kind, place] = part[place * 2 + row, :, :cut]
            advance(kind, a_sum.at[kind], a_side.at[kind], place)
    a_across = copies.start(a_sum.at[0, outer], a_take, partner)
    for at in range(line):
        place = goal(at)
        across[at].wait_recv()
        b_sum[place] = add(b_sum[place], part[place * 2 + inner, :, cut:])
        advance(2, b_sum, b_side, place)

    def shift(column, source, land):
        return pltpu.make_async_remote_copy(
            src_ref=source,
            dst_ref=land,
            send_sem=shift_send.at[column],
            recv_sem=shift_recv.at[column],
            device_id={"section": (section + sections - 1) % sections},
            device_id_type=MESH,
        )

    a_across.wait_recv()
    a_sum[1, outer] = add(a_sum[1, outer], a_take[...])
    shifts = (shift(0, a_sum.at[1, outer], land_a), shift(1, b_sum.at[outer], land_b))

    @pl.when(section > 0)
    def _():
        for copy in shifts:
            copy.start()

    for copy in tiny:
        copy.wait_recv()
    copies.finish()
    for place in range(line):
        for kind, total, side_ref in (
            (0, a_sum.at[0], a_side.at[0]),
            (1, a_sum.at[1], a_side.at[1]),
            (2, b_sum, b_side),
        ):
            guarded(place > outer, line_copy(kind, total, side_ref, 0, place).wait_send)
            guarded(place < outer, line_copy(kind, total, side_ref, 1, place).wait_send)

    @pl.when(section > 0)
    def _():
        for copy in shifts:
            copy.wait_send()

    @pl.when(section < sections - 1)
    def _():
        shifts[0].wait_recv()
        out[:, :cut] = land_a[...]
        shifts[1].wait_recv()
        out[:, cut:] = land_b[...]

    @pl.when(section == sections - 1)
    def _():
        out[...] = jnp.zeros_like(out)


def scatter_tokens(count, sections, part, prob):
    pairs = scatter_copies(count)
    line = count // 2
    _, tokens, width = part.shape
    cut = max(width // 1024, 1) * 128
    rest = width - cut
    return pl.pallas_call(
        functools.partial(scatter_kernel, count, sections),
        out_shape=[
            jax.ShapeDtypeStruct((tokens, width), BF16),
            jax.ShapeDtypeStruct(prob.shape, prob.dtype),
        ],
        in_specs=[VMEM] * 2,
        out_specs=[VMEM] * 2,
        scratch_shapes=[
            pltpu.VMEM((2, line, tokens, cut), BF16),
            pltpu.VMEM((2, 2, line, tokens, cut), BF16),
            pltpu.VMEM((tokens, cut), BF16),
            pltpu.VMEM((line, tokens, rest), BF16),
            pltpu.VMEM((2, line, tokens, rest), BF16),
            pltpu.VMEM((tokens, cut), BF16),
            pltpu.VMEM((tokens, rest), BF16),
            pltpu.SemaphoreType.DMA((pairs,)),
            pltpu.SemaphoreType.DMA((pairs,)),
            pltpu.SemaphoreType.DMA((3, 2, line)),
            pltpu.SemaphoreType.DMA((3, 2, line)),
            pltpu.SemaphoreType.DMA((2,)),
            pltpu.SemaphoreType.DMA((2,)),
        ],
        compiler_params=pltpu.CompilerParams(
            collective_id=1, has_side_effects=True, vmem_limit_bytes=48 * 1024 * 1024
        ),
    )(part, prob)


def per_device(
    output_grad,
    layer_input,
    expert_ids,
    route_probs,
    gate_weight,
    up_weight,
    down_weight,
    saved_inputs,
    saved_gate_grad,
    saved_up_grad,
    saved_counts,
):
    ep_count = lax.axis_size("ep")
    sections = lax.axis_size("section")
    me = lax.axis_index("ep")
    w_gate = gate_weight[0]
    w_up = up_weight[0]
    w_down = down_weight[0]
    local_experts = w_gate.shape[0]
    experts_all = local_experts * ep_count
    slots_all = saved_inputs.shape[2]
    capacity = slots_all // ep_count
    tok_rows = expert_ids.shape[1]
    top_count = expert_ids.shape[2]
    width = output_grad.shape[2]

    small = jnp.concatenate([expert_ids[0].astype(BF16), route_probs[0]], axis=1).T
    live = jnp.arange(capacity, dtype=jnp.int32)[None, None, :] < saved_counts[0][:, :, None]
    live = jnp.broadcast_to(
        live.reshape(local_experts, slots_all, 1).astype(BF16), (local_experts, slots_all, 128)
    )
    grad_all, input_all, small_all, gate_part, up_part = gather_tokens(
        ep_count,
        output_grad[0],
        layer_input[0],
        small,
        live,
        saved_inputs[0],
        saved_gate_grad[0],
        saved_up_grad[0],
    )

    ids_all = small_all[:, :top_count].astype(jnp.int32)
    probs_all = small_all[:, top_count:].astype(F32)
    mine = me * local_experts + jnp.arange(local_experts, dtype=jnp.int32)
    hit = ids_all[:, None, :, :] == mine[None, :, None, None]
    member = jnp.any(hit, axis=2)
    prob = jnp.sum(jnp.where(hit, probs_all[:, None], 0.0), axis=2)
    lower = jnp.tril(jnp.ones((tok_rows, tok_rows), BF16), -1)
    before = jnp.einsum("sen,tn->set", member.astype(BF16), lower, preferred_element_type=F32)
    slot = jnp.where(member, before.astype(jnp.int32), -1)
    chosen = slot[:, :, None, :] == jnp.arange(capacity, dtype=jnp.int32)[None, None, :, None]
    pick = chosen.astype(BF16).reshape(ep_count, local_experts * capacity, tok_rows)
    put = jnp.where(chosen, prob[:, :, None, :], 0.0).astype(BF16)
    put = put.reshape(ep_count, local_experts * capacity, tok_rows)

    def spread(tokens):
        sent = jnp.einsum("spt,std->spd", pick, tokens, preferred_element_type=F32).astype(BF16)
        sent = sent.reshape(ep_count, local_experts, capacity, width)
        return sent.transpose(1, 0, 2, 3).reshape(local_experts, slots_all, width)

    grad_part = spread(grad_all)
    input_part = spread(input_all)

    gate_pre = jnp.einsum("epd,edf->epf", input_part, w_gate, preferred_element_type=F32)
    up_pre = jnp.einsum("epd,edf->epf", input_part, w_up, preferred_element_type=F32)
    sigma = jax.nn.sigmoid(gate_pre)
    active = gate_pre * sigma
    hidden = active * up_pre
    hidden_grad = jnp.einsum("epd,efd->epf", grad_part, w_down, preferred_element_type=F32)
    slot_prob = jnp.sum(hidden_grad * hidden, axis=2).astype(BF16)
    gate_grad = (hidden_grad * up_pre * sigma * (1.0 + gate_pre * (1.0 - sigma))).astype(BF16)
    up_grad = (hidden_grad * active).astype(BF16)
    slot_grad = jnp.einsum("epf,edf->epd", gate_grad, w_gate, preferred_element_type=F32)
    slot_grad = slot_grad + jnp.einsum("epf,edf->epd", up_grad, w_up, preferred_element_type=F32)
    slot_grad = slot_grad.astype(BF16).reshape(local_experts, ep_count, capacity, width)
    slot_grad = slot_grad.transpose(1, 0, 2, 3).reshape(ep_count, -1, width)
    token_grad = jnp.einsum("spt,spd->std", put, slot_grad, preferred_element_type=F32)
    slot_prob = slot_prob.reshape(local_experts, ep_count, capacity)
    by_slot = chosen.astype(BF16)
    token_prob = jnp.einsum("sect,esc->set", by_slot, slot_prob, preferred_element_type=F32)
    upstream, prob_back = scatter_tokens(
        ep_count, sections, token_grad.astype(BF16), token_prob.astype(BF16)
    )
    prob_back = prob_back.reshape(experts_all, tok_rows)
    own = expert_ids[0][None, :, :] == jnp.arange(experts_all, dtype=jnp.int32)[:, None, None]
    prob_part = jnp.sum(jnp.where(own, prob_back[:, :, None].astype(F32), 0.0), axis=0)
    prob_part = prob_part.astype(BF16)
    upstream = upstream[None]
    return (upstream, prob_part[None], gate_part[None], up_part[None])


def solution(mesh):
    three = P("section", "ep", None)
    four = P("section", "ep", None, None)
    return jax.shard_map(
        per_device,
        mesh=mesh,
        in_specs=(three, three, three, three, four, four, four, four, four, four, three),
        out_specs=(three, three, four, four),
        check_vma=False,
    )
```

profile of v0, /device:TPU:9, one launch (start us, length us, event | category | flops | bytes accessed | tf_op | source)
XLA Modules:
  0.0 238.7 jit_solution(17428005532707007544)
XLA Ops:
  0.6 0.9 lt.30
  1.7 0.4 broadcast_in_dim.72.live
  2.1 0.7 bitcast_convert_fusion.1
  2.8 0.7 maximum_bitcast_fusion.s
  3.5 1.5 copy-done.3
  5.1 1.5 copy-done.4
  6.6 1.0 copy-done.5
  7.7 1.0 copy-done.6
  8.7 88.0 %shard_map.138 = (bf16[8,256,1024]{2,1,0:T(8,128)(2,1)}, bf16[8,256,1024]{2,1,0:T(8,128)(2,1)}, bf16[8,16,256]{2,1,0:T(8,128)(2,1)S(1)}, bf16[4,1024,384]{2,1,0:T(8,128)(2,1)}, bf16[4,1024,384]{2,1,0:T(8,128)(2,1)}) custom-call(bf16[256,1024]{1,0:T(8,128)(2,1)S(1)} %bitcast.69, bf16[256,1024]{1,0:T(8,128)(2,1)S(1)} %bitcast.70, ...), custom_call_target="tpu_custom_call" | custom-call | tf_op jit(solution)/shard_map/pallas_call | solution.py:180
  96.7 0.2 compare_reduce_fusion
  96.9 0.2 fusion.14
  97.3 0.4 bitcast_compare_fusion
  97.7 3.7 %convolution_convert_fusion = bf16[8,320,1024]{2,1,0:T(8,128)(2,1)S(1)} fusion(pred[8,320,256]{2,1,0:T(32,128)(4,1)S(1)} %bitcast_compare_fusion, bf16[8,256,1024]{2,1,0:T(8,128)(2,1)} %get-tuple-element.13), kind=kOutput, calls=%fused_computation.15 | convolution fusion | flops 1344798720 | bytes 10092544 | tf_op jit(solution)/shard_map/spt,std->spd/dot_general | solution.py:428
  101.5 0.9 copy.28
  102.4 2.8 %fusion.3 = f32[4,640,384]{1,2,0:T(8,128)S(1)} fusion(bf16[4,640,1024]{2,1,0:T(8,128)(2,1)S(1)} %bitcast.79, bf16[1,4,1024,384]{3,2,1,0:T(8,128)(2,1)S(1)} %copy-done), kind=kOutput, calls=%fused_computation.8 | convolution fusion | flops 2013265920 | bytes 12320768 | tf_op jit(solution)/shard_map/epd,edf->epf/dot_general | solution.py:435
  105.3 4.9 %fusion.6 = f32[4,640,384]{1,2,0:T(8,128)} fusion(bf16[4,640,1024]{2,1,0:T(8,128)(2,1)S(1)} %bitcast.80, bf16[1,4,1024,384]{3,2,1,0:T(8,128)(2,1)S(1)} %copy-done.11), kind=kOutput, calls=%fused_computation.11 | convolution fusion | flops 2013265920 | bytes 12320768 | tf_op jit(solution)/shard_map/epd,edf->epf/dot_general | solution.py:436
  110.1 1.5 convolution_convert_fusion.1
  111.7 0.9 copy.27
  112.6 0.9 copy-done.10
  113.6 6.3 %multiply_reduce_fusion = (bf16[4,640]{1,0:T(4,128)(2,1)S(1)}, f32[4,640,384]{1,2,0:T(8,128)}) fusion(f32[4,640,384]{1,2,0:T(8,128)} %fusion.6, f32[4,640,384]{1,2,0:T(8,128)S(1)} %fusion.3, bf16[4,640,1024]{2,1,0:T(8,128)(2,1)S(1)} %bitcast.77, bf16[1,4,384,1024]{3,2,1,0:T(8,128)(2,1)S(1)} %copy-done.10), kind=kOutput, calls=%fused_computation.1 | convolution fusion | flops 2020144640 | bytes 20190208 | tf_op jit(solution)/shard_map/epd,efd->epf/dot_general | solution.py:440
  119.9 11.2 %fusion.1 = f32[4,640,1024]{2,1,0:T(8,128)} fusion(bf16[1,4,1024,384]{3,2,1,0:T(8,128)(2,1)S(1)} %copy-done, f32[4,640,384]{1,2,0:T(8,128)S(1)} %fusion.3, f32[4,640,384]{1,2,0:T(8,128)} %get-tuple-element.21, f32[4,640,384]{1,2,0:T(8,128)} %fusion.6), kind=kOutput, calls=%fused_computation.6 | convolution fusion | flops 2023096320 | bytes 25427968 | tf_op jit(solution)/shard_map/epf,edf->epd/dot_general | solution.py:444
  131.1 13.0 %add_convert_fusion = bf16[4,640,1024]{2,1,0:T(8,128)(2,1)} fusion(f32[4,640,1024]{2,1,0:T(8,128)} %fusion.1, bf16[1,4,1024,384]{3,2,1,0:T(8,128)(2,1)} %param.16, f32[4,640,384]{1,2,0:T(8,128)} %get-tuple-element.21, f32[4,640,384]{1,2,0:T(8,128)} %copy-done.12), kind=kOutput, calls=%fused_computation | convolution fusion | flops 2024407040 | bytes 26738688 | tf_op jit(solution)/shard_map/epf,edf->epd/dot_general | solution.py:445
  144.1 3.2 %copy.33 = bf16[8,4,80,1024]{3,2,1,0:T(8,128)(2,1)S(1)} copy(bf16[8,4,80,1024]{3,2,0,1:T(8,128)(2,1)} %bitcast.78) | data formatting | bytes 10485760 | tf_op jit(solution)/shard_map/transpose | solution.py:447
  147.5 0.3 fusion.10
  147.8 4.3 %convolution_convert_fusion.2.part = bf16[8,256,1024]{2,1,0:T(8,128)(2,1)} fusion(bf16[8,320,256]{2,1,0:T(8,128)(2,1)S(1)} %fusion.10, bf16[8,320,1024]{2,1,0:T(8,128)(2,1)S(1)} %bitcast.73), kind=kOutput, calls=%fused_computation.17 | convolution fusion | flops 1344274432 | bytes 10747904 | tf_op jit(solution)/shard_map/spt,spd->std/dot_general | solution.py:448
  152.2 0.5 fusion.11
  152.7 2.2 copy-done.2
  154.9 76.6 %shard_map.139 = (bf16[256,1024]{1,0:T(8,128)(2,1)S(1)}, bf16[8,4,256]{2,1,0:T(4,128)(2,1)S(1)}) custom-call(bf16[8,256,1024]{2,1,0:T(8,128)(2,1)S(1)} %copy-done.2, bf16[8,4,256]{2,1,0:T(4,128)(2,1)S(1)} %bitcast.72), custom_call_target="tpu_custom_call" | custom-call | tf_op jit(solution)/shard_map/pallas_call | solution.py:341
  231.6 0.6 select_reduce_fusion
  232.2 0.8 copy.52
  233.0 4.0 %copy.53 = bf16[1,4,1024,384]{3,2,1,0:T(8,128)(2,1)} copy(bf16[1,4,1024,384]{3,2,1,0:T(8,128)(2,1)} %bitcast.82) | data formatting | bytes 6291456
  237.0 1.7 copy.54
  (34 shorter events, 0.6 us)
Async XLA Ops:
  0.6 101.8 %copy-start = (bf16[1,4,1024,384]{3,2,1,0:T(8,128)(2,1)S(1)}, bf16[1,4,1024,384]{3,2,1,0:T(8,128)(2,1)}, u32[]{:S(2)}) copy-start(bf16[1,4,1024,384]{3,2,1,0:T(8,128)(2,1)} %param.15) | copy-start | bytes 9437188
  3.5 1.5 copy-start.3
  5.1 1.5 copy-start.4
  6.6 1.0 copy-start.5
  7.7 1.0 copy-start.6
  102.4 2.9 %copy-start.11 = (bf16[1,4,1024,384]{3,2,1,0:T(8,128)(2,1)S(1)}, bf16[1,4,1024,384]{3,2,1,0:T(8,128)(2,1)}, u32[]{:S(2)}) copy-start(bf16[1,4,1024,384]{3,2,1,0:T(8,128)(2,1)} %param.16) | copy-start | bytes 9437188
  105.3 14.6 %copy-start.12 = (f32[4,640,384]{1,2,0:T(8,128)}, f32[4,640,384]{1,2,0:T(8,128)S(1)}, u32[]{:S(2)}) copy-start(f32[4,640,384]{1,2,0:T(8,128)S(1)} %fusion.3) | copy-start | bytes 11796484
  105.3 4.9 %copy-start.7 = (bf16[8,256,1024]{2,1,0:T(8,128)(2,1)S(1)}, bf16[8,256,1024]{2,1,0:T(8,128)(2,1)}, u32[]{:S(2)}) copy-start(bf16[8,256,1024]{2,1,0:T(8,128)(2,1)} %get-tuple-element.12) | copy-start | bytes 12582916
  111.7 1.9 copy-start.10
  152.1 79.4 %copy-start.9 = (s32[1,256,8]{1,2,0:T(8,128)S(1)}, s32[1,256,8]{1,2,0:T(8,128)}, u32[]{:S(2)}) copy-start(s32[1,256,8]{1,2,0:T(8,128)} %param.13) | copy-start | bytes 24580
  152.7 2.2 copy-start.2
  231.5 5.5 %copy-start.8 = (bf16[4,1024,384]{2,1,0:T(8,128)(2,1)S(1)}, bf16[4,1024,384]{2,1,0:T(8,128)(2,1)}, u32[]{:S(2)}) copy-start(bf16[4,1024,384]{2,1,0:T(8,128)(2,1)} %get-tuple-element.17) | copy-start | bytes 9437188
  233.0 5.7 %copy-start.1 = (bf16[1,4,1024,384]{3,2,1,0:T(8,128)(2,1)S(1)}, bf16[1,4,1024,384]{3,2,1,0:T(8,128)(2,1)}, u32[]{:S(2)}) copy-start(bf16[1,4,1024,384]{3,2,1,0:T(8,128)(2,1)} %param.15) | copy-start | bytes 9437188
where the time goes:
time: 239 us
  Pallas kernels  165 us (69%)
  matrix products  48.5 us (20%)
  local copies, waits for them, and re-layouts  21.6 us (9%)
  other arithmetic  3.1 us (1%)
    pallas_call x1, Pallas kernels, gather_tokens(): pl.pallas_call(functools.partial(gather_kernel, count), out_shape=[jax.Sh...  88 us
    pallas_call x1, Pallas kernels, scatter_tokens(): pl.pallas_call(functools.partial(scatter_kernel, count, sections), out_sh...  76.6 us
    unnamed x29, local copies, waits for them, and re-layouts  14.8 us
    dot_general x1, matrix products, per_device(): jnp.einsum('epf,edf->epd', up_grad, w_up, preferred_element_type=F32)  13 us
    dot_general x1, matrix products, per_device(): jnp.einsum('epf,edf->epd', gate_grad, w_gate, preferred_element_type=F32)  11.2 us
    dot_general x1, matrix products, per_device(): jnp.einsum('epd,efd->epf', grad_part, w_down, preferred_element_type=F32)  6.27 us
    dot_general x2, matrix products, spread(): jnp.einsum('spt,std->spd', pick, tokens, preferred_element_type=F32)  5.26 us
    dot_general x1, matrix products, per_device(): jnp.einsum('epd,edf->epf', input_part, w_up, preferred_element_type=F32)  4.85 us

commit v1 on v0

v1 whole, which is shorter than its diff:
```python
import functools

import jax
import jax.numpy as jnp
from jax import lax
from jax.experimental import pallas as pl
from jax.experimental.pallas import tpu as pltpu
from jax.sharding import PartitionSpec as P

F32 = jnp.float32
BF16 = jnp.bfloat16
MESH = pl.DeviceIdType.MESH
VMEM = pl.BlockSpec(memory_space=pltpu.VMEM)
SMEM = pl.BlockSpec(memory_space=pltpu.SMEM)
ANY = pl.BlockSpec(memory_space=pl.ANY)
TILE = 256


def guarded(when, act):
    if when is None:
        act()
    else:
        pl.when(when)(act)


def both(a, b):
    return jnp.logical_and(a, b)


def add(a, b):
    return (a.astype(F32) + b.astype(F32)).astype(BF16)


def dot(a, b, dims):
    return lax.dot_general(a, b, (dims, ((), ())), preferred_element_type=F32)


def cuts(width):
    return max(width * 3 // 1024, 1) * 128, max(width // 1024, 1) * 128


def fused_kernel(
    count, sections, cap,
    g, x, ids, probs, counts, gate_w, up_w, down_w, held_in, gate_in, up_in,
    out, prob_out, gate_out, up_out,
    x_all, g_all, s_all, w_in, w_down, held, gate_held, up_held, gate_stage, up_stage,
    slots, weights, rows, keep_hidden, keep_active, keep_gate, back, part, prob_part, prob_in,
    a_sum, a_side, a_take, b_sum, b_take, b_side, land_a, land_b,
    own_sem, load_sem, held_sem, stage_sem, s_send, s_recv, z_send, z_recv, y_send, y_recv,
    o_send, o_recv, p_send, p_recv, c_send, c_recv, line_send, line_recv, shift_send, shift_recv,
):
    me = lax.axis_index("ep")
    section = lax.axis_index("section")
    outer, inner = me // 2, me % 2
    other = 1 - inner
    line = count // 2
    up = ((outer + 1) % line) * 2 + inner
    down = ((outer + line - 1) % line) * 2 + inner
    sides = (up, down)
    partner = outer * 2 + other
    experts = gate_w.shape[0]
    tokens, width = g.shape
    hidden = gate_w.shape[2]
    top = ids.shape[0]
    padded = rows.shape[1] // 2
    slot_rows = held_in.shape[1]
    cut, low_cut = cuts(width)
    everything, few, many = pl.ds(0, width), pl.ds(0, cut), pl.ds(cut, width - cut)
    side_list = (0, 1)

    def remote(src, dst, send, recv, target):
        return pltpu.make_async_remote_copy(
            src_ref=src, dst_ref=dst, send_sem=send, recv_sem=recv, device_id=target,
            device_id_type=MESH,
        )

    own = [
        pltpu.make_async_copy(g, g_all.at[me], own_sem.at[0]),
        pltpu.make_async_copy(x, x_all.at[me], own_sem.at[1]),
    ]
    for copy in own:
        copy.start()

    def held_loads(expert, at):
        return [
            pltpu.make_async_copy(src.at[expert], dst.at[at], held_sem.at[kind, at])
            for kind, (src, dst) in enumerate(
                ((held_in, held), (gate_in, gate_held), (up_in, up_held))
            )
        ]

    for expert in range(min(2, experts)):
        for copy in held_loads(expert, expert):
            copy.start()
    loads = [
        pltpu.make_async_copy(gate_w, w_in.at[:, :, pl.ds(0, hidden)], load_sem.at[0]),
        pltpu.make_async_copy(up_w, w_in.at[:, :, pl.ds(hidden, hidden)], load_sem.at[1]),
        pltpu.make_async_copy(down_w, w_down, load_sem.at[2]),
    ]
    for copy in loads:
        copy.start()

    s_all[me] = jnp.concatenate([ids[...].astype(F32), probs[...].astype(F32)], axis=0).astype(BF16)

    barrier = pltpu.get_barrier_semaphore()
    for away in range(1, count):
        pl.semaphore_signal(
            barrier, inc=1, device_id={"ep": (me + away) % count}, device_id_type=MESH
        )
    for away in (1, sections - 1):
        pl.semaphore_signal(
            barrier, inc=1, device_id={"section": (section + away) % sections}, device_id_type=MESH
        )
    for copy in own:
        copy.wait()
    pl.semaphore_wait(barrier, count + 1)

    def s_copy(away):
        return remote(
            s_all.at[me], s_all.at[me], s_send.at[away - 1], s_recv.at[away - 1],
            {"ep": (me + away) % count},
        )

    for away in range(1, count):
        s_copy(away).start()

    def block(step, side):
        return (outer + (-step if side == 0 else step) + 2 * line) % line

    def arrives(step, side):
        return outer >= step + 1 if side == 0 else outer + step + 1 <= line - 1

    def leaves(step, side):
        if side == 0:
            return both(outer >= step, outer < line - 1)
        return both(outer + step <= line - 1, outer > 0)

    pieces = ((x_all, everything), (g_all, many), (g_all, few), (g_all, few))

    def z_copy(at, side, step):
        ref, columns = pieces[at]
        spot = ref.at[block(step, side) * 2 + (other if at == 3 else inner), :, columns]
        return remote(
            spot, spot, z_send.at[at, side, step], z_recv.at[at, side, step], {"ep": sides[side]}
        )

    def y_copy(at, side, step):
        ref, columns = pieces[at]
        spot = ref.at[block(step + 1, side) * 2 + inner, :, columns]
        return remote(
            spot, spot, y_send.at[at, side, step], y_recv.at[at, side, step], {"ep": partner}
        )

    def o_copy(at):
        ref, columns = pieces[at]
        spot = ref.at[me, :, columns]
        return remote(spot, spot, o_send.at[at], o_recv.at[at], {"ep": partner})

    o_copy(2).start()
    for at in range(3):
        for side in side_list:
            pl.when(leaves(0, side))(z_copy(at, side, 0).start)
    o_copy(0).start()
    o_copy(1).start()

    def weight_expert(expert, carry):
        at = expert % 2
        for copy in held_loads(expert, at):
            copy.wait()
        place = lax.broadcasted_iota(jnp.int32, (slot_rows, 128), 0)
        live = jnp.zeros((slot_rows, 128), F32)
        for source in range(count):
            low = source * cap
            inside = both(place >= low, place < low + counts[expert, source])
            live = jnp.where(inside, 1.0, live)
        live = live.astype(BF16)
        for ref in (gate_held, up_held):
            for group in range(hidden // 128):
                columns = pl.ds(group * 128, 128)
                ref[at, :, columns] = ref[at, :, columns] * live

        def stage_copies(old):
            return [
                pltpu.make_async_copy(stage.at[at], dst.at[old], stage_sem.at[kind, at])
                for kind, (stage, dst) in enumerate(((gate_stage, gate_out), (up_stage, up_out)))
            ]

        @pl.when(expert >= 2)
        def _():
            for copy in stage_copies(expert - 2):
                copy.wait()

        def body(tile, carry):
            columns = pl.ds(pl.multiple_of(tile * TILE, TILE), TILE)
            some = held[at, :, columns]
            for ref, stage in ((gate_held, gate_stage), (up_held, up_stage)):
                stage[at, columns, :] = dot(some, ref[at], ((0,), (0,))).astype(BF16)
            return carry

        lax.fori_loop(0, width // TILE, body, 0)
        for copy in stage_copies(expert):
            copy.start()

        @pl.when(expert + 2 < experts)
        def _():
            for copy in held_loads(expert + 2, at):
                copy.start()

        return carry

    def weight_finish():
        for expert in range(max(experts - 2, 0), experts):
            for kind, (stage, dst) in enumerate(((gate_stage, gate_out), (up_stage, up_out))):
                pltpu.make_async_copy(
                    stage.at[expert % 2], dst.at[expert], stage_sem.at[kind, expert % 2]
                ).wait()

    def route():
        members = []
        for source in range(count):
            named = s_all[source].astype(F32)
            chosen, prob = named[:top], named[top:]
            for expert in range(experts):
                hit = chosen == (me * experts + expert).astype(F32)
                members.append(jnp.max(jnp.where(hit, 1.0, 0.0), axis=0, keepdims=True))
                weights[source, expert] = jnp.sum(jnp.where(hit, prob, 0.0), axis=0, keepdims=True)
        member = jnp.concatenate(members, axis=0)
        earlier = lax.broadcasted_iota(jnp.int32, (tokens, tokens), 0) < lax.broadcasted_iota(
            jnp.int32, (tokens, tokens), 1
        )
        before = dot(
            member.astype(BF16), jnp.where(earlier, 1.0, 0.0).astype(BF16), ((1,), (0,))
        )
        slot = jnp.where(member > 0.5, before, -1.0)
        for source in range(count):
            for expert in range(experts):
                at = source * experts + expert
                slots[source, expert] = slot[at : at + 1]

    spots = lax.broadcasted_iota(jnp.int32, (padded, tokens), 0).astype(F32)

    def picked(source, scaled):
        parts = []
        for expert in range(experts):
            value = weights[source, expert] if scaled else 1.0
            parts.append(jnp.where(spots == slots[source, expert], value, 0.0).astype(BF16))
        return jnp.concatenate(parts, axis=0)

    def spread(unit, ref):
        for row in range(2):
            source = unit * 2 + row
            pick = picked(source, False)
            for tile in range(width // TILE):
                columns = pl.ds(tile * TILE, TILE)
                got = dot(pick, ref[source, :, columns], ((1,), (0,))).astype(BF16)
                for expert in range(experts):
                    rows[expert, pl.ds(row * padded, padded), columns] = got[
                        expert * padded : (expert + 1) * padded
                    ]

    def forward(unit, side):
        spread(unit, x_all)

        def body(expert, carry):
            pre = dot(rows[expert], w_in[expert], ((1,), (0,)))
            gate, upper = pre[:, :hidden], pre[:, hidden:]
            sigma = jax.nn.sigmoid(gate)
            active = gate * sigma
            keep_active[side, expert] = active
            keep_hidden[side, expert] = active * upper
            keep_gate[side, expert] = upper * sigma * (1.0 + gate * (1.0 - sigma))
            return carry

        lax.fori_loop(0, experts, body, 0)

    def backward(unit, side):
        spread(unit, g_all)

        def body(expert, carry):
            grad = dot(rows[expert], w_down[expert], ((1,), (1,)))
            score = jnp.sum(grad * keep_hidden[side, expert], axis=1, keepdims=True)
            score = score.astype(BF16).astype(F32)
            pre_grad = jnp.concatenate(
                [
                    (grad * keep_gate[side, expert]).astype(BF16),
                    (grad * keep_active[side, expert]).astype(BF16),
                ],
                axis=1,
            )
            for tile in range(width // TILE):
                columns = pl.ds(tile * TILE, TILE)
                sent = dot(pre_grad, w_in[expert, columns, :], ((1,), (1,))).astype(BF16)
                for row in range(2):
                    back[
                        row, pl.ds(pl.multiple_of(expert * padded, padded), padded), columns
                    ] = sent[row * padded : (row + 1) * padded]
            for row in range(2):
                source = unit * 2 + row
                mine = jnp.where(
                    spots == slots[source, expert], score[row * padded : (row + 1) * padded], 0.0
                )
                prob_part[source, expert] = jnp.sum(mine, axis=0, keepdims=True)
            return carry

        lax.fori_loop(0, experts, body, 0)
        for row in range(2):
            source = unit * 2 + row
            put = picked(source, True)
            for tile in range(width // TILE):
                columns = pl.ds(tile * TILE, TILE)
                part[source, :, columns] = dot(put, back[row, :, columns], ((0,), (0,))).astype(BF16)

    def valid(step, side):
        if side == 0:
            return outer >= step + 1
        return both(outer + step + 1 <= line - 1, step >= 0)

    def unit_loop(step, act, at):
        def body(side, carry):
            unit = (outer + jnp.where(side == 0, -step - 1, step + 1) + 2 * line) % line
            ok = jnp.where(
                side == 0,
                jnp.where(outer >= step + 1, 1, 0),
                jnp.where(both(outer + step + 1 <= line - 1, step >= 0), 1, 0),
            )

            @pl.when(ok == 1)
            def _():
                act(unit, side)

            return carry

        for side in side_list:
            @pl.when(both(valid(step, side), step >= 0))
            def _(side=side):
                y_copy(at, side, step).wait_recv()

        @pl.when(step < 0)
        def _():
            o_copy(at).wait_recv()

        lax.fori_loop(0, 2, body, 0)

    def take(at, step):
        for side in side_list:
            pl.when(arrives(step, side))(z_copy(at, side, step).wait_recv)

            @pl.when(both(leaves(step + 1, side), step < line - 2))
            def _(side=side):
                z_copy(at, side, step + 1).start()

            if at < 2:
                pl.when(arrives(step, side))(y_copy(at, side, step).start)

    def turn(index, carry):
        step = index - 1
        moving = both(step >= 0, step < line - 1)
        first = jnp.where(index == 0, 0, jnp.minimum(index + 1, experts))
        last = jnp.minimum(index + 2, experts)
        lax.fori_loop(first, last, weight_expert, 0)

        @pl.when(moving)
        def _():
            take(0, step)
            take(1, step)

        @pl.when(step >= 0)
        def _():
            unit_loop(step - 1, backward, 1)

        @pl.when(both(step >= 0, step < line - 2))
        def _():
            take(2, step)
            take(3, step)

        @pl.when(step < line - 1)
        def _():
            unit_loop(step, forward, 0)

        @pl.when(step == line - 2)
        def _():
            take(2, step)
            take(3, step)

        return carry

    for away in range(1, count):
        s_copy(away).wait_recv()
    o_copy(2).wait_recv()
    for side in side_list:
        pl.when(leaves(0, side))(z_copy(3, side, 0).start)
    route()
    for copy in loads:
        copy.wait()
    lax.fori_loop(0, line + 1, turn, 0)
    if experts > line + 2:
        lax.fori_loop(line + 2, experts, weight_expert, 0)

    low, high = pl.ds(0, low_cut), pl.ds(low_cut, width - low_cut)

    def goal(at):
        mixed = line - 1 - at // 2 if at % 2 == 0 else at // 2
        return jnp.where(outer == 0, line - 1 - at, jnp.where(outer == line - 1, at, mixed))

    def across(at):
        return remote(
            part.at[goal(at) * 2 + other, :, high], b_take.at[goal(at)], c_send.at[at],
            c_recv.at[at], {"ep": partner},
        )

    def p_copy(away):
        target = (me + away) % count
        return remote(
            prob_part.at[target], prob_in.at[me], p_send.at[away - 1], p_recv.at[away - 1],
            {"ep": target},
        )

    for at in range(line):
        across(at).start()
    for away in range(1, count):
        p_copy(away).start()
    prob_in[me] = prob_part[me]

    def line_copy(kind, source, side_ref, side, place, spot):
        return remote(
            source.at[place], side_ref.at[spot], line_send.at[kind, side, place],
            line_recv.at[kind, side, place], {"ep": sides[side]},
        )

    def spot_of(side, place, where):
        return jnp.where(place == where, line, place) if side == 1 else place

    def collect(kind, total, side_ref, side, place):
        spot = spot_of(side, place, outer)
        line_copy(kind, total, side_ref, side, place, spot).wait_recv()
        total[place] = add(total[place], side_ref[spot])

    def advance(kind, total, side_ref, place):
        @pl.when(both(place >= outer, outer > 0))
        def _():
            collect(kind, total, side_ref, 0, place)

        @pl.when(both(place <= outer, outer < line - 1))
        def _():
            collect(kind, total, side_ref, 1, place)

        @pl.when(place > outer)
        def _():
            line_copy(kind, total, side_ref, 0, place, spot_of(0, place, outer + 1)).start()

        @pl.when(place < outer)
        def _():
            line_copy(kind, total, side_ref, 1, place, spot_of(1, place, outer - 1)).start()

    a_across = remote(
        a_sum.at[0, outer], a_take, c_send.at[line], c_recv.at[line], {"ep": partner}
    )
    for at in range(line):
        place = goal(at)
        for kind, row in ((0, other), (1, inner)):
            a_sum[kind, place] = part[place * 2 + row, :, :low_cut]
            advance(kind, a_sum.at[kind], a_side.at[kind], place)
    a_across.start()
    for at in range(line):
        place = goal(at)
        across(at).wait_recv()
        b_sum[place] = add(b_take[place], part[place * 2 + inner, :, low_cut:])
        advance(2, b_sum, b_side, place)

    def shift(column, source, land):
        return remote(
            source, land, shift_send.at[column], shift_recv.at[column],
            {"section": (section + sections - 1) % sections},
        )

    a_across.wait_recv()
    a_sum[1, outer] = add(a_sum[1, outer], a_take[...])
    shifts = (shift(0, a_sum.at[1, outer], land_a), shift(1, b_sum.at[outer], land_b))

    @pl.when(section > 0)
    def _():
        for copy in shifts:
            copy.start()

    for away in range(1, count):
        p_copy(away).wait_recv()
    total = jnp.zeros((top, tokens), F32)
    for expert in range(experts * count):
        value = prob_in[expert // experts, expert % experts]
        total = jnp.where(ids[...] == expert, value, total)
    prob_out[...] = total.astype(BF16)
    weight_finish()

    for away in range(1, count):
        s_copy(away).wait_send()
        p_copy(away).wait_send()
    for at in range(3):
        o_copy(at).wait_send()

    def drain(step, carry):
        for side in side_list:
            for at in range(4):
                pl.when(leaves(step, side))(z_copy(at, side, step).wait_send)
            for at in range(2):
                pl.when(arrives(step, side))(y_copy(at, side, step).wait_send)
        return carry

    lax.fori_loop(0, line - 1, drain, 0)
    for at in range(line):
        across(at).wait_send()
    a_across.wait_send()
    for place in range(line):
        for kind, source, side_ref in (
            (0, a_sum.at[0], a_side.at[0]), (1, a_sum.at[1], a_side.at[1]), (2, b_sum, b_side),
        ):
            pl.when(place > outer)(line_copy(kind, source, side_ref, 0, place, place).wait_send)
            pl.when(place < outer)(line_copy(kind, source, side_ref, 1, place, place).wait_send)

    @pl.when(section > 0)
    def _():
        for copy in shifts:
            copy.wait_send()

    @pl.when(section < sections - 1)
    def _():
        shifts[0].wait_recv()
        out[:, :low_cut] = land_a[...]
        shifts[1].wait_recv()
        out[:, low_cut:] = land_b[...]

    @pl.when(section == sections - 1)
    def _():
        out[...] = jnp.zeros_like(out)


def fused(count, sections, g, x, ids, probs, counts, gate_w, up_w, down_w, held, gate, up):
    line = count // 2
    tokens, width = g.shape
    experts, _, hidden = gate_w.shape
    top = ids.shape[0]
    slot_rows = held.shape[1]
    cap = slot_rows // count
    padded = -(-cap // 16) * 16
    _, low_cut = cuts(width)
    rest = width - low_cut
    dma = pltpu.SemaphoreType.DMA
    grads = jax.ShapeDtypeStruct((experts, width, hidden), BF16)
    return pl.pallas_call(
        functools.partial(fused_kernel, count, sections, cap),
        out_shape=[
            jax.ShapeDtypeStruct((tokens, width), BF16),
            jax.ShapeDtypeStruct((top, tokens), BF16),
            grads,
            grads,
        ],
        in_specs=[ANY, ANY, VMEM, VMEM, SMEM] + [ANY] * 6,
        out_specs=[VMEM, VMEM, ANY, ANY],
        scratch_shapes=[
            pltpu.VMEM((count, tokens, width), BF16),
            pltpu.VMEM((count, tokens, width), BF16),
            pltpu.VMEM((count, 2 * top, tokens), BF16),
            pltpu.VMEM((experts, width, 2 * hidden), BF16),
            pltpu.VMEM((experts, hidden, width), BF16),
            pltpu.VMEM((2, slot_rows, width), BF16),
            pltpu.VMEM((2, slot_rows, hidden), BF16),
            pltpu.VMEM((2, slot_rows, hidden), BF16),
            pltpu.VMEM((2, width, hidden), BF16),
            pltpu.VMEM((2, width, hidden), BF16),
            pltpu.VMEM((count, experts, 1, tokens), F32),
            pltpu.VMEM((count, experts, 1, tokens), F32),
            pltpu.VMEM((experts, 2 * padded, width), BF16),
            pltpu.VMEM((2, experts, 2 * padded, hidden), F32),
            pltpu.VMEM((2, experts, 2 * padded, hidden), F32),
            pltpu.VMEM((2, experts, 2 * padded, hidden), F32),
            pltpu.VMEM((2, experts * padded, width), BF16),
            pltpu.VMEM((count, tokens, width), BF16),
            pltpu.VMEM((count, experts, 1, tokens), F32),
            pltpu.VMEM((count, experts, 1, tokens), F32),
            pltpu.VMEM((2, line, tokens, low_cut), BF16),
            pltpu.VMEM((2, line + 1, tokens, low_cut), BF16),
            pltpu.VMEM((tokens, low_cut), BF16),
            pltpu.VMEM((line, tokens, rest), BF16),
            pltpu.VMEM((line, tokens, rest), BF16),
            pltpu.VMEM((line + 1, tokens, rest), BF16),
            pltpu.VMEM((tokens, low_cut), BF16),
            pltpu.VMEM((tokens, rest), BF16),
            dma((2,)),
            dma((3,)),
            dma((3, 2)),
            dma((2, 2)),
            dma((count - 1,)),
            dma((count - 1,)),
            dma((4, 2, line - 1)),
            dma((4, 2, line - 1)),
            dma((2, 2, line - 1)),
            dma((2, 2, line - 1)),
            dma((3,)),
            dma((3,)),
            dma((count - 1,)),
            dma((count - 1,)),
            dma((line + 1,)),
            dma((line + 1,)),
            dma((3, 2, line)),
            dma((3, 2, line)),
            dma((2,)),
            dma((2,)),
        ],
        compiler_params=pltpu.CompilerParams(
            collective_id=0, has_side_effects=True, vmem_limit_bytes=63 * 1024 * 1024
        ),
    )(g, x, ids, probs, counts, gate_w, up_w, down_w, held, gate, up)


def publish_kernel(top, gate, up, out, gate_out, up_out, held, read, write):
    moves = []
    for source, goal in ((top, out), (gate, gate_out), (up, up_out)):
        half = source.shape[0] // 2
        for part in range(2):
            moves.append((source.at[pl.ds(part * half, half)], goal.at[pl.ds(part * half, half)]))
    spots = [held[at // 2].at[at % 2] for at in range(len(moves))]
    reads = [
        pltpu.make_async_copy(source, spot, read.at[at])
        for at, ((source, _), spot) in enumerate(zip(moves, spots))
    ]
    writes = [
        pltpu.make_async_copy(spot, goal, write.at[at])
        for at, ((_, goal), spot) in enumerate(zip(moves, spots))
    ]
    for copy in reads:
        copy.start()
    for before, after in zip(reads, writes):
        before.wait()
        after.start()
    for copy in writes:
        copy.wait()


def publish(top, gate, up):
    arrays = (top, gate, up)

    def kernel(a, b, c, d, e, f, h0, h1, h2, read, write):
        publish_kernel(a, b, c, d, e, f, (h0, h1, h2), read, write)

    return pl.pallas_call(
        kernel,
        out_shape=[jax.ShapeDtypeStruct(a.shape, a.dtype) for a in arrays],
        in_specs=[ANY] * 3,
        out_specs=[ANY] * 3,
        scratch_shapes=[
            pltpu.VMEM((2, a.shape[0] // 2) + a.shape[1:], a.dtype) for a in arrays
        ] + [pltpu.SemaphoreType.DMA((6,)), pltpu.SemaphoreType.DMA((6,))],
    )(*arrays)


def per_device(
    output_grad,
    layer_input,
    expert_ids,
    route_probs,
    gate_weight,
    up_weight,
    down_weight,
    saved_inputs,
    saved_gate_grad,
    saved_up_grad,
    saved_counts,
):
    upstream, prob, gate_part, up_part = fused(
        lax.axis_size("ep"),
        lax.axis_size("section"),
        output_grad[0],
        layer_input[0],
        expert_ids[0].T,
        route_probs[0].T,
        saved_counts[0],
        gate_weight[0],
        up_weight[0],
        down_weight[0],
        saved_inputs[0],
        saved_gate_grad[0],
        saved_up_grad[0],
    )
    upstream, gate_part, up_part = publish(upstream, gate_part, up_part)
    return (upstream[None], prob.T[None], gate_part[None], up_part[None])


def solution(mesh):
    three = P("section", "ep", None)
    four = P("section", "ep", None, None)
    return jax.shard_map(
        per_device,
        mesh=mesh,
        in_specs=(three, three, three, three, four, four, four, four, four, four, three),
        out_specs=(three, three, four, four),
        check_vma=False,
    )
```

time: 239 us -> 176 us (0.74)
  matrix products: 48.5 us -> 0 us
  local copies, waits for them, and re-layouts: 21.6 us -> 0.6 us
  Pallas kernels: 165 us -> 175 us
  other arithmetic: 3.1 us -> 0 us
    dot_general x10 -> x0, matrix products: 48.5 us -> none  [the longest x1 13 us: per_device(): jnp.einsum('epf,edf->epd', up_grad, w_up, preferred_element_type=F32)]
    unnamed x29 -> x3, local copies, waits for them, and re-layouts: 14.8 us -> 0.6 us
    pallas_call x2, Pallas kernels: 165 us -> 175 us  [the longest x1 169 us: fused(): pl.pallas_call(functools.partial(fused_kernel, count, sections, cap), out...]
    transpose x3 -> x0, local copies, waits for them, and re-layouts: 5.07 us -> none  [the longest x1 3.23 us: per_device(): slot_grad = slot_grad.transpose(1, 0, 2, 3).reshape(ep_count, -1, width)]
where the time goes in v1:
time: 176 us
  Pallas kernels  175 us (99%)
    pallas_call x1, Pallas kernels, fused(): pl.pallas_call(functools.partial(fused_kernel, count, sections, cap), out...  169 us
    pallas_call x1, Pallas kernels, publish(): pl.pallas_call(kernel, out_shape=[jax.ShapeDtypeStruct(a.shape, a.dtype)...  5.95 us

profile of v1, /device:TPU:9, one launch (start us, length us, event | category | flops | bytes accessed | tf_op | source)
XLA Modules:
  0.0 176.0 jit_solution(13024963359512521581)
XLA Ops:
  0.6 168.8 %shard_map.138 = (bf16[256,1024]{1,0:T(8,128)(2,1)}, bf16[8,256]{1,0:T(8,128)(2,1)}, bf16[4,1024,384]{2,1,0:T(8,128)(2,1)}, bf16[4,1024,384]{2,1,0:T(8,128)(2,1)}) custom-call(bf16[256,1024]{1,0:T(8,128)(2,1)} %bitcast.27, bf16[256,1024]{1,0:T(8,128)(2,1)} %bitcast.28, s32[8,256]{1,0:T(8,128)} %bitcast.29, bf16[8,256]{1,0:T(8,128)(2,1)} %bitcast.31, ...), custom_call_target="tpu_custom_call" | custom-call | tf_op jit(solution)/shard_map/pallas_call | solution.py:548
  169.4 0.0 copy-start
  169.4 6.0 %shard_map.139 = (bf16[256,1024]{1,0:T(8,128)(2,1)}, bf16[4,1024,384]{2,1,0:T(8,128)(2,1)}, bf16[4,1024,384]{2,1,0:T(8,128)(2,1)}) custom-call(bf16[256,1024]{1,0:T(8,128)(2,1)} %get-tuple-element.11.a, bf16[4,1024,384]{2,1,0:T(8,128)(2,1)} %get-tuple-element.12.b, bf16[4,1024,384]{2,1,0:T(8,128)(2,1)} %get-tuple-element.13.c), custom_call_target="tpu_custom_call" | custom-call | tf_op jit(solution)/shard_map/pallas_call | solution.py:644
  175.4 0.0 copy-done
  175.4 0.6 copy.16
Async XLA Ops:
  169.4 6.0 %copy-start = (bf16[8,256]{1,0:T(8,128)(2,1)S(1)}, bf16[8,256]{1,0:T(8,128)(2,1)}, u32[]{:S(2)}) copy-start(bf16[8,256]{1,0:T(8,128)(2,1)} %get-tuple-element.15) | copy-start | bytes 12292

commit v2 on v1

v2 whole, which is shorter than its diff:
```python
import functools

import jax
import jax.numpy as jnp
from jax import lax
from jax.experimental import pallas as pl
from jax.experimental.pallas import tpu as pltpu
from jax.sharding import PartitionSpec as P

F32 = jnp.float32
BF16 = jnp.bfloat16
MESH = pl.DeviceIdType.MESH
VMEM = pl.BlockSpec(memory_space=pltpu.VMEM)
SMEM = pl.BlockSpec(memory_space=pltpu.SMEM)
ANY = pl.BlockSpec(memory_space=pl.ANY)
HBM = pl.BlockSpec(memory_space=pltpu.HBM)
TILE = 256
PIECES = 2


def guarded(when, act):
    if when is None:
        act()
    else:
        pl.when(when)(act)


def both(a, b):
    return jnp.logical_and(a, b)


def add(a, b):
    return (a.astype(F32) + b.astype(F32)).astype(BF16)


def dot(a, b, dims):
    return lax.dot_general(a, b, (dims, ((), ())), preferred_element_type=F32)


def cut_of(width):
    return max(width * 5 // 1024, 1) * 128


def fused_kernel(
    count, sections, cap, roomy,
    g, x, ids, probs, counts, gate_w, up_w, down_w, held_in, gate_in, up_in,
    out, prob_out, gate_out, up_out,
    x_all, g_all, s_all, w_in, w_down, held, gate_held, up_held, gate_stage, up_stage,
    slots, weights, rows, keep_hidden, keep_active, keep_gate, back, part, prob_part, prob_in,
    chain_in, cross_in, end_in, end_sum, final_in,
    own_sem, load_sem, held_sem, stage_sem, s_send, s_recv, z_send, z_recv, y_send, y_recv,
    o_send, o_recv, p_send, p_recv, chain_send, chain_recv, cross_send, cross_recv, end_send,
    end_recv, final_send, final_recv, shift_send, shift_recv,
):
    me = lax.axis_index("ep")
    section = lax.axis_index("section")
    outer, inner = me // 2, me % 2
    other = 1 - inner
    line = count // 2
    up = ((outer + 1) % line) * 2 + inner
    down = ((outer + line - 1) % line) * 2 + inner
    sides = (up, down)
    partner = outer * 2 + other
    experts = gate_w.shape[0]
    tokens, width = g.shape
    hidden = gate_w.shape[2]
    top = ids.shape[0]
    padded = rows.shape[1] // 2
    slot_rows = held_in.shape[1]
    cut = cut_of(width)
    everything, few, many = pl.ds(0, width), pl.ds(0, cut), pl.ds(cut, width - cut)
    side_list = (0, 1)

    def remote(src, dst, send, recv, target):
        return pltpu.make_async_remote_copy(
            src_ref=src, dst_ref=dst, send_sem=send, recv_sem=recv, device_id=target,
            device_id_type=MESH,
        )

    own = [
        pltpu.make_async_copy(g, g_all.at[me], own_sem.at[0]),
        pltpu.make_async_copy(x, x_all.at[me], own_sem.at[1]),
    ]
    for copy in own:
        copy.start()

    def held_loads(expert, at):
        return [
            pltpu.make_async_copy(src.at[expert], dst.at[at], held_sem.at[kind, at])
            for kind, (src, dst) in enumerate(
                ((held_in, held), (gate_in, gate_held), (up_in, up_held))
            )
        ]

    s_all[me] = jnp.concatenate([ids[...].astype(F32), probs[...].astype(F32)], axis=0).astype(BF16)

    barrier = pltpu.get_barrier_semaphore()
    for away in range(1, count):
        pl.semaphore_signal(
            barrier, inc=1, device_id={"ep": (me + away) % count}, device_id_type=MESH
        )
    for away in (1, sections - 1):
        pl.semaphore_signal(
            barrier, inc=1, device_id={"section": (section + away) % sections}, device_id_type=MESH
        )
    pl.semaphore_wait(barrier, count + 1)

    def s_copy(away):
        return remote(
            s_all.at[me], s_all.at[me], s_send.at[away - 1], s_recv.at[away - 1],
            {"ep": (me + away) % count},
        )

    for away in range(1, count):
        s_copy(away).start()

    def block(step, side):
        return (outer + (-step if side == 0 else step) + 2 * line) % line

    def arrives(step, side):
        return outer >= step + 1 if side == 0 else outer + step + 1 <= line - 1

    def leaves(step, side):
        if side == 0:
            return both(outer >= step, outer < line - 1)
        return both(outer + step <= line - 1, outer > 0)

    pieces = ((x_all, everything), (g_all, many), (g_all, few), (g_all, few))

    def z_copy(at, side, step, source=None):
        ref, columns = pieces[at]
        spot = ref.at[block(step, side) * 2 + (other if at == 3 else inner), :, columns]
        return remote(
            spot if source is None else source.at[:, columns], spot, z_send.at[at, side, step],
            z_recv.at[at, side, step], {"ep": sides[side]},
        )

    def y_copy(at, side, step):
        ref, columns = pieces[at]
        spot = ref.at[block(step + 1, side) * 2 + inner, :, columns]
        return remote(
            spot, spot, y_send.at[at, side, step], y_recv.at[at, side, step], {"ep": partner}
        )

    def o_copy(at):
        ref, columns = pieces[at]
        spot = ref.at[me, :, columns]
        return remote(
            (x, g, g)[at].at[:, columns], spot, o_send.at[at], o_recv.at[at], {"ep": partner}
        )

    o_copy(2).start()
    for at in range(3):
        for side in side_list:
            pl.when(leaves(0, side))(z_copy(at, side, 0, (x, g, g)[at]).start)
    o_copy(0).start()
    o_copy(1).start()
    for expert in range(min(2, experts)):
        for copy in held_loads(expert, expert):
            copy.start()
    loads = [
        pltpu.make_async_copy(gate_w, w_in.at[:, :, pl.ds(0, hidden)], load_sem.at[0]),
        pltpu.make_async_copy(up_w, w_in.at[:, :, pl.ds(hidden, hidden)], load_sem.at[1]),
        pltpu.make_async_copy(down_w, w_down, load_sem.at[2]),
    ]
    for copy in loads:
        copy.start()


    def hop_of(side):
        return outer + 1 if side == 0 else outer - 1

    def chain(block_at, side, row, at, where):
        rows_at = pl.ds(at * (tokens // PIECES), tokens // PIECES)
        spot = jnp.where(block_at == where, line - 2, block_at - 1) if side == 1 else block_at - 1
        return remote(
            part.at[block_at * 2 + row, rows_at], chain_in.at[spot, row, rows_at],
            chain_send.at[block_at - 1, side, row, at], chain_recv.at[block_at - 1, side, row, at],
            {"ep": sides[side]},
        )

    def weight_expert(expert, carry):
        at = expert % 2
        for copy in held_loads(expert, at):
            copy.wait()
        place = lax.broadcasted_iota(jnp.int32, (slot_rows, 128), 0)
        live = jnp.zeros((slot_rows, 128), F32)
        for source in range(count):
            low = source * cap
            inside = both(place >= low, place < low + counts[expert, source])
            live = jnp.where(inside, 1.0, live)
        live = live.astype(BF16)
        for ref in (gate_held, up_held):
            for group in range(hidden // 128):
                columns = pl.ds(group * 128, 128)
                ref[at, :, columns] = ref[at, :, columns] * live

        def stage_copies(old):
            return [
                pltpu.make_async_copy(stage.at[at], dst.at[old], stage_sem.at[kind, at])
                for kind, (stage, dst) in enumerate(((gate_stage, gate_out), (up_stage, up_out)))
            ]

        if not roomy:
            @pl.when(expert >= 2)
            def _():
                for copy in stage_copies(expert - 2):
                    copy.wait()

        goals = (gate_out, up_out) if roomy else (gate_stage, up_stage)
        place_at = expert if roomy else at

        def body(tile, carry):
            columns = pl.ds(pl.multiple_of(tile * TILE, TILE), TILE)
            some = held[at, :, columns]
            for ref, stage in zip((gate_held, up_held), goals):
                stage[place_at, columns, :] = dot(some, ref[at], ((0,), (0,))).astype(BF16)
            return carry

        lax.fori_loop(0, width // TILE, body, 0)
        if not roomy:
            for copy in stage_copies(expert):
                copy.start()

        @pl.when(expert + 2 < experts)
        def _():
            for copy in held_loads(expert + 2, at):
                copy.start()

        return carry

    def weight_finish():
        if roomy:
            return
        for expert in range(max(experts - 2, 0), experts):
            for kind, (stage, dst) in enumerate(((gate_stage, gate_out), (up_stage, up_out))):
                pltpu.make_async_copy(
                    stage.at[expert % 2], dst.at[expert], stage_sem.at[kind, expert % 2]
                ).wait()

    def route():
        members = []
        for source in range(count):
            named = s_all[source].astype(F32)
            chosen, prob = named[:top], named[top:]
            for expert in range(experts):
                hit = chosen == (me * experts + expert).astype(F32)
                members.append(jnp.max(jnp.where(hit, 1.0, 0.0), axis=0, keepdims=True))
                weights[source, expert] = jnp.sum(jnp.where(hit, prob, 0.0), axis=0, keepdims=True)
        member = jnp.concatenate(members, axis=0)
        earlier = lax.broadcasted_iota(jnp.int32, (tokens, tokens), 0) < lax.broadcasted_iota(
            jnp.int32, (tokens, tokens), 1
        )
        before = dot(
            member.astype(BF16), jnp.where(earlier, 1.0, 0.0).astype(BF16), ((1,), (0,))
        )
        slot = jnp.where(member > 0.5, before, -1.0)
        for source in range(count):
            for expert in range(experts):
                at = source * experts + expert
                slots[source, expert] = slot[at : at + 1]

    spots = lax.broadcasted_iota(jnp.int32, (padded, tokens), 0).astype(F32)

    def picked(source, scaled):
        parts = []
        for expert in range(experts):
            value = weights[source, expert] if scaled else 1.0
            parts.append(jnp.where(spots == slots[source, expert], value, 0.0).astype(BF16))
        return jnp.concatenate(parts, axis=0)

    def spread(unit, ref):
        for row in range(2):
            source = unit * 2 + row
            pick = picked(source, False)
            for tile in range(width // TILE):
                columns = pl.ds(tile * TILE, TILE)
                got = dot(pick, ref[source, :, columns], ((1,), (0,))).astype(BF16)
                for expert in range(experts):
                    rows[expert, pl.ds(row * padded, padded), columns] = got[
                        expert * padded : (expert + 1) * padded
                    ]

    def forward(unit, side):
        spread(unit, x_all)

        def body(expert, carry):
            pre = dot(rows[expert], w_in[expert], ((1,), (0,)))
            gate, upper = pre[:, :hidden], pre[:, hidden:]
            sigma = jax.nn.sigmoid(gate)
            active = gate * sigma
            keep_active[side, expert] = active
            keep_hidden[side, expert] = active * upper
            keep_gate[side, expert] = upper * sigma * (1.0 + gate * (1.0 - sigma))
            return carry

        lax.fori_loop(0, experts, body, 0)

    def backward(unit, side):
        spread(unit, g_all)

        def body(expert, carry):
            grad = dot(rows[expert], w_down[expert], ((1,), (1,)))
            score = jnp.sum(grad * keep_hidden[side, expert], axis=1, keepdims=True)
            score = score.astype(BF16).astype(F32)
            pre_grad = jnp.concatenate(
                [
                    (grad * keep_gate[side, expert]).astype(BF16),
                    (grad * keep_active[side, expert]).astype(BF16),
                ],
                axis=1,
            )
            for tile in range(width // TILE):
                columns = pl.ds(tile * TILE, TILE)
                sent = dot(pre_grad, w_in[expert, columns, :], ((1,), (1,))).astype(BF16)
                for row in range(2):
                    back[
                        row, pl.ds(pl.multiple_of(expert * padded, padded), padded), columns
                    ] = sent[row * padded : (row + 1) * padded]
            for row in range(2):
                source = unit * 2 + row
                mine = jnp.where(
                    spots == slots[source, expert], score[row * padded : (row + 1) * padded], 0.0
                )
                prob_part[source, expert] = jnp.sum(mine, axis=0, keepdims=True)
            return carry

        lax.fori_loop(0, experts, body, 0)
        for row in range(2):
            source = unit * 2 + row
            put = picked(source, True)
            for tile in range(width // TILE):
                columns = pl.ds(tile * TILE, TILE)
                sent = dot(put, back[row, :, columns], ((0,), (0,)))
                part[source, :, columns] = sent.astype(BF16)
        within = both(unit > 0, unit < line - 1)
        for way, edge in ((0, 0), (1, line - 1)):
            @pl.when(both(outer == edge, within))
            def _(way=way, edge=edge):
                split = unit == (line - 2 if edge == 0 else 1)
                for at in range(PIECES):
                    for row in range(2):
                        send = chain(unit, way, row, at, hop_of(way)).start
                        if at < PIECES // 2:
                            send()
                        else:
                            pl.when(jnp.logical_not(split))(send)

    def unit_turn(step, side, act, at):
        unit = (outer + (-step - 1 if side == 0 else step + 1) + 2 * line) % line
        own_turn = step < 0
        later = both(arrives(step, side), step >= 0)
        pl.when(later)(y_copy(at, side, step).wait_recv)
        if side == 0:
            pl.when(own_turn)(o_copy(at).wait_recv)

        @pl.when(jnp.logical_or(later, own_turn) if side == 0 else later)
        def _():
            act(unit, side)

    def take(at, step):
        for side in side_list:
            pl.when(arrives(step, side))(z_copy(at, side, step).wait_recv)

            @pl.when(both(leaves(step + 1, side), step < line - 2))
            def _(side=side):
                z_copy(at, side, step + 1).start()

            if at < 2:
                pl.when(arrives(step, side))(y_copy(at, side, step).start)

    at_end = jnp.logical_or(outer == 0, outer == line - 1)

    def turn(index, carry):
        step = index - 1
        early = both(step >= 0, step < line - 2)
        pl.when(early)(lambda: take(0, step))
        pl.when(both(early, index == 1))(lambda: take(1, step))

        @pl.when(index < 2)
        def _():
            experts_of(index)

        @pl.when(step >= 0)
        def _():
            unit_turn(step - 1, 0, backward, 1)
            unit_turn(step - 1, 1, backward, 1)

        pl.when(both(early, index > 1))(lambda: take(1, step))

        @pl.when(index >= 2)
        def _():
            experts_of(index)

        @pl.when(step == line - 2)
        def _():
            take(0, step)
            take(1, step)
            chain_start(range(PIECES // 2, PIECES))

        @pl.when(early)
        def _():
            take(2, step)
            take(3, step)

        @pl.when(step < line - 1)
        def _():
            unit_turn(step, 0, forward, 0)
            unit_turn(step, 1, forward, 0)

        @pl.when(step == line - 2)
        def _():
            take(2, step)
            take(3, step)

        return carry

    def experts_of(index):
        first = jnp.where(index == 0, 0, jnp.minimum(index + 1, experts))
        last = jnp.minimum(index + 2, experts)
        lax.fori_loop(first, last, weight_expert, 0)

    def chain_start(some):
        for way, edge, unit in ((0, 0, line - 2), (1, line - 1, 1)):
            @pl.when(outer == edge)
            def _(way=way, unit=unit):
                for at in some:
                    for row in range(2):
                        chain(unit, way, row, at, hop_of(way)).start()

    for away in range(1, count):
        s_copy(away).wait_recv()
    route()
    for copy in own:
        copy.wait()
    o_copy(2).wait_recv()
    for side in side_list:
        pl.when(leaves(0, side))(z_copy(3, side, 0).start)
    for copy in loads:
        copy.wait()
    lax.fori_loop(0, line + 1, turn, 0)
    if experts > line + 2:
        lax.fori_loop(line + 2, experts, weight_expert, 0)

    span = tokens // PIECES
    far = jnp.where(outer < line // 2, line - 1, 0)
    near = line - 1 - far
    far_end, near_end = far // (line - 1), near // (line - 1)
    far_side = jnp.where(outer < line // 2, up, down)
    near_side = jnp.where(outer < line // 2, down, up)

    def chunk(at):
        return pl.ds(at * span, span)

    def p_copy(away):
        target = (me + away) % count
        return remote(
            prob_part.at[target], prob_in.at[me], p_send.at[away - 1], p_recv.at[away - 1],
            {"ep": target},
        )

    def cross(block_at, end, at):
        return remote(
            part.at[block_at * 2 + other, chunk(at)], cross_in.at[end, chunk(at)],
            cross_send.at[end, at], cross_recv.at[end, at], {"ep": partner},
        )

    def final(at):
        return remote(
            part.at[outer * 2 + other, chunk(at)], final_in.at[chunk(at)], final_send.at[at],
            final_recv.at[at], {"ep": partner},
        )

    def end_copy(end, at, target):
        return remote(
            end_sum.at[end, chunk(at)], end_in.at[end, chunk(at)], end_send.at[end, at],
            end_recv.at[end, at], {"ep": target},
        )

    def shift(source, at):
        return remote(
            source, out.at[chunk(at)], shift_send.at[at], shift_recv.at[at],
            {"section": (section + sections - 1) % sections},
        )

    for away in range(1, count):
        p_copy(away).start()
    prob_in[me] = prob_part[me]
    ends = ((far, far_end), (near, near_end))
    in_turn = [(end, at) for end in range(2) for at in range(PIECES)]
    mixed_up = [(end, at) for at in range(PIECES) for end in range(2)]

    def crossing(order):
        for end, piece in order:
            cross(*ends[end], piece).start()

    def end_step(order, place, target):
        is_far, at = order[place][0] == 0, order[place][1]
        block_at, end = ends[order[place][0]]
        cross(block_at, end, at).wait_recv()
        rows_at = chunk(at)
        total = part[block_at * 2 + inner, rows_at].astype(F32) + cross_in[end, rows_at].astype(F32)
        end_sum[end, rows_at] = total.astype(BF16)
        first = jnp.logical_or(outer == 0, outer == line - 1) if is_far else None

        def gather_in():
            end_copy(end, at, target).wait_recv()
            end_sum[end, rows_at] = add(end_sum[end, rows_at], end_in[end, rows_at])

        if is_far:
            pl.when(jnp.logical_not(first))(gather_in)
            end_copy(end, at, target).start()
        else:
            gather_in()

    @pl.when(at_end)
    def _():
        crossing(in_turn[:PIECES])
        for at in range(PIECES):
            end_step(in_turn, at, far_side)
        crossing(in_turn[PIECES:])
        for at in range(PIECES):
            end_step(in_turn, PIECES + at, near_side)

            @pl.when(section > 0)
            def _(at=at):
                shift(end_sum.at[near_end, chunk(at)], at).start()

    @pl.when(jnp.logical_not(at_end))
    def _():
        crossing(mixed_up)
        order = []
        for half in range((line - 1) // 2):
            order += [line - 2 - half] + ([1 + half] if 1 + half != line - 2 - half else [])
        for block_at in order:
            for side in side_list:
                @pl.when(block_at > outer if side == 0 else block_at < outer)
                def _(block_at=block_at, side=side):
                    for at in range(PIECES):
                        for row in range(2):
                            chain(block_at, side, row, at, outer).wait_recv()
                            spot = block_at * 2 + row
                            part[spot, chunk(at)] = add(
                                part[spot, chunk(at)], chain_in[block_at - 1, row, chunk(at)]
                            )
                            chain(block_at, side, row, at, hop_of(side)).start()
        for at in range(PIECES):
            end_step(mixed_up, 2 * at, far_side)
            end_step(mixed_up, 2 * at + 1, near_side)
            end_copy(near_end, at, near_side).start()
            for row in range(2):
                for side in side_list:
                    chain(outer, side, row, at, outer).wait_recv()
                spot = outer * 2 + row
                total = part[spot, chunk(at)].astype(F32)
                total = total + chain_in[outer - 1, row, chunk(at)].astype(F32)
                total = total + chain_in[line - 2, row, chunk(at)].astype(F32)
                part[spot, chunk(at)] = total.astype(BF16)
            final(at).start()
        for at in range(PIECES):
            final(at).wait_recv()
            spot = outer * 2 + inner
            part[spot, chunk(at)] = add(part[spot, chunk(at)], final_in[chunk(at)])

            @pl.when(section > 0)
            def _(at=at):
                shift(part.at[outer * 2 + inner, chunk(at)], at).start()

    for away in range(1, count):
        p_copy(away).wait_recv()
    total = jnp.zeros((top, tokens), F32)
    for expert in range(experts * count):
        value = prob_in[expert // experts, expert % experts]
        total = jnp.where(ids[...] == expert, value, total)
    prob_out[...] = total.astype(BF16)
    weight_finish()

    for away in range(1, count):
        s_copy(away).wait_send()
        p_copy(away).wait_send()
    for at in range(3):
        o_copy(at).wait_send()

    def drain(step, carry):
        for side in side_list:
            for at in range(4):
                pl.when(leaves(step, side))(z_copy(at, side, step).wait_send)
            for at in range(2):
                pl.when(arrives(step, side))(y_copy(at, side, step).wait_send)
        return carry

    lax.fori_loop(0, line - 1, drain, 0)
    for at in range(PIECES):
        cross(far, far_end, at).wait_send()
        cross(near, near_end, at).wait_send()
        end_copy(far_end, at, far_side).wait_send()

        @pl.when(jnp.logical_not(at_end))
        def _(at=at):
            end_copy(near_end, at, near_side).wait_send()
            final(at).wait_send()

    for block_at in range(1, line - 1):
        for side in side_list:
            @pl.when(block_at > outer if side == 0 else block_at < outer)
            def _(block_at=block_at, side=side):
                for at in range(PIECES):
                    for row in range(2):
                        chain(block_at, side, row, at, hop_of(side)).wait_send()

    @pl.when(section > 0)
    def _():
        for at in range(PIECES):
            shift(end_sum.at[0, chunk(at)], at).wait_send()

    @pl.when(section < sections - 1)
    def _():
        for at in range(PIECES):
            shift(end_sum.at[0, chunk(at)], at).wait_recv()

    @pl.when(section == sections - 1)
    def _():
        out[...] = jnp.zeros_like(out)


def fused(count, sections, g, x, ids, probs, counts, gate_w, up_w, down_w, held, gate, up):
    line = count // 2
    tokens, width = g.shape
    experts, _, hidden = gate_w.shape
    top = ids.shape[0]
    slot_rows = held.shape[1]
    cap = slot_rows // count
    padded = -(-cap // 16) * 16
    dma = pltpu.SemaphoreType.DMA
    roomy = is_roomy(count, tokens, width)
    stage = (1, 16, 128) if roomy else (2, width, hidden)
    results = [(tokens, width), (top, tokens), (experts, width, hidden), (experts, width, hidden)]
    return pl.pallas_call(
        functools.partial(fused_kernel, count, sections, cap, roomy),
        out_shape=[
            pltpu.VMEM(shape, BF16) if roomy else jax.ShapeDtypeStruct(shape, BF16)
            for shape in results
        ],
        in_specs=[HBM, HBM, VMEM, VMEM, SMEM] + [HBM] * 6,
        out_specs=[VMEM, VMEM] + [VMEM if roomy else HBM] * 2,
        scratch_shapes=[
            pltpu.VMEM((count, tokens, width), BF16),
            pltpu.VMEM((count, tokens, width), BF16),
            pltpu.VMEM((count, 2 * top, tokens), BF16),
            pltpu.VMEM((experts, width, 2 * hidden), BF16),
            pltpu.VMEM((experts, hidden, width), BF16),
            pltpu.VMEM((2, slot_rows, width), BF16),
            pltpu.VMEM((2, slot_rows, hidden), BF16),
            pltpu.VMEM((2, slot_rows, hidden), BF16),
            pltpu.VMEM(stage, BF16),
            pltpu.VMEM(stage, BF16),
            pltpu.VMEM((count, experts, 1, tokens), F32),
            pltpu.VMEM((count, experts, 1, tokens), F32),
            pltpu.VMEM((experts, 2 * padded, width), BF16),
            pltpu.VMEM((2, experts, 2 * padded, hidden), F32),
            pltpu.VMEM((2, experts, 2 * padded, hidden), F32),
            pltpu.VMEM((2, experts, 2 * padded, hidden), F32),
            pltpu.VMEM((2, experts * padded, width), BF16),
            pltpu.VMEM((count, tokens, width), BF16),
            pltpu.VMEM((count, experts, 1, tokens), F32),
            pltpu.VMEM((count, experts, 1, tokens), F32),
            pltpu.VMEM((line - 1, 2, tokens, width), BF16),
            pltpu.VMEM((2, tokens, width), BF16),
            pltpu.VMEM((2, tokens, width), BF16),
            pltpu.VMEM((2, tokens, width), BF16),
            pltpu.VMEM((tokens, width), BF16),
            dma((2,)),
            dma((3,)),
            dma((3, 2)),
            dma((2, 2)),
            dma((count - 1,)),
            dma((count - 1,)),
            dma((4, 2, line - 1)),
            dma((4, 2, line - 1)),
            dma((2, 2, line - 1)),
            dma((2, 2, line - 1)),
            dma((3,)),
            dma((3,)),
            dma((count - 1,)),
            dma((count - 1,)),
            dma((line - 2, 2, 2, PIECES)),
            dma((line - 2, 2, 2, PIECES)),
            dma((2, PIECES)),
            dma((2, PIECES)),
            dma((2, PIECES)),
            dma((2, PIECES)),
            dma((PIECES,)),
            dma((PIECES,)),
            dma((PIECES,)),
            dma((PIECES,)),
        ],
        compiler_params=pltpu.CompilerParams(
            collective_id=0, has_side_effects=True,
            vmem_limit_bytes=(48 if roomy else 63) * 1024 * 1024,
        ),
    )(g, x, ids, probs, counts, gate_w, up_w, down_w, held, gate, up)


def is_roomy(count, tokens, width):
    return count * tokens * width <= 2 * 1024 * 1024


def publish(direct, arrays):
    total = len(arrays)

    def kernel(*refs):
        sources, goals, held = refs[:total], refs[total : 2 * total], refs[2 * total : -2]
        read, write = refs[-2:]
        moves = []
        for source, goal, spot in zip(sources, goals, held):
            if len(source.shape) == 2:
                moves.append((source, goal, spot))
        for at in range(sources[-1].shape[0]):
            for source, goal, spot in zip(sources, goals, held):
                if len(source.shape) == 3:
                    moves.append((source.at[at], goal.at[at], spot.at[at]))
        def move(at, source, goal, sems):
            return pltpu.make_async_copy(source, goal, sems.at[at])

        for at, (source, goal, spot) in enumerate(moves):
            if direct:
                move(at, source, goal, write).start()
            else:
                move(at, source, spot, read).start()
        for at, (source, goal, spot) in enumerate(moves):
            if not direct:
                move(at, source, spot, read).wait()
                move(at, spot, goal, write).start()
        for at, (source, goal, spot) in enumerate(moves):
            move(at, source if direct else spot, goal, write).wait()

    pieces = sum(a.shape[0] if len(a.shape) == 3 else 1 for a in arrays)
    return pl.pallas_call(
        kernel,
        out_shape=[jax.ShapeDtypeStruct(a.shape, a.dtype) for a in arrays],
        in_specs=[VMEM if direct else ANY] * total,
        out_specs=[HBM] * total,
        scratch_shapes=[
            pltpu.VMEM((8,) * (len(a.shape) - 1) + (128,) if direct else a.shape, a.dtype)
            for a in arrays
        ]
        + [pltpu.SemaphoreType.DMA((pieces,))] * 2,
        compiler_params=pltpu.CompilerParams(vmem_limit_bytes=(4 if direct else 32) * 1024 * 1024),
    )(*arrays)


def per_device(
    output_grad,
    layer_input,
    expert_ids,
    route_probs,
    gate_weight,
    up_weight,
    down_weight,
    saved_inputs,
    saved_gate_grad,
    saved_up_grad,
    saved_counts,
):
    upstream, prob, gate_part, up_part = fused(
        lax.axis_size("ep"),
        lax.axis_size("section"),
        output_grad[0],
        layer_input[0],
        expert_ids[0].T,
        route_probs[0].T,
        saved_counts[0],
        gate_weight[0],
        up_weight[0],
        down_weight[0],
        saved_inputs[0],
        saved_gate_grad[0],
        saved_up_grad[0],
    )
    direct = is_roomy(lax.axis_size("ep"), output_grad.shape[1], output_grad.shape[2])
    upstream, prob, gate_part, up_part = publish(direct, (upstream, prob, gate_part, up_part))
    return (upstream[None], prob.T[None], gate_part[None], up_part[None])


def solution(mesh):
    three = P("section", "ep", None)
    four = P("section", "ep", None, None)
    return jax.shard_map(
        per_device,
        mesh=mesh,
        in_specs=(three, three, three, three, four, four, four, four, four, four, three),
        out_specs=(three, three, four, four),
        check_vma=False,
    )
```

time: 176 us -> 145 us (0.82)
  Pallas kernels: 175 us -> 143 us
    pallas_call x1, Pallas kernels: 169 us -> 140 us  [fused(): pl.pallas_call(functools.partial(fused_kernel, count, sections, cap, room...]
    pallas_call x1, Pallas kernels: 5.95 us -> 3 us  [publish(): pl.pallas_call(kernel, out_shape=[jax.ShapeDtypeStruct(a.shape, a.dtype)...]
where the time goes in v2:
time: 145 us; the launch traced here: 144 us
  Pallas kernels  143 us (99%)
    pallas_call x1, Pallas kernels, fused(): pl.pallas_call(functools.partial(fused_kernel, count, sections, cap, room...  140 us
    pallas_call x1, Pallas kernels, publish(): pl.pallas_call(kernel, out_shape=[jax.ShapeDtypeStruct(a.shape, a.dtype)...  3 us

profile of v2, /device:TPU:9, one launch (start us, length us, event | category | flops | bytes accessed | tf_op | source)
XLA Modules:
  0.0 143.9 jit_solution(15960099162246470056)
XLA Ops:
  0.6 140.3 %shard_map.138 = (bf16[256,1024]{1,0:T(8,128)(2,1)S(1)}, bf16[8,256]{1,0:T(8,128)(2,1)S(1)}, bf16[4,1024,384]{2,1,0:T(8,128)(2,1)S(1)}, bf16[4,1024,384]{2,1,0:T(8,128)(2,1)S(1)}) custom-call(bf16[256,1024]{1,0:T(8,128)(2,1)} %bitcast.27, bf16[256,1024]{1,0:T(8,128)(2,1)} %bitcast.28, s32[8,256]{1,0:T(8,128)} %bitcast.29, bf16[8,256]{1,0:T(8,128)(2,1)} %bitcast.30, ...), custom_call_target="tpu_custom_call" | custom-call | tf_op jit(solution)/shard_map/pallas_call | solution.py:638
  140.9 3.0 %shard_map.139 = (bf16[256,1024]{1,0:T(8,128)(2,1)}, bf16[8,256]{1,0:T(8,128)(2,1)}, bf16[4,1024,384]{2,1,0:T(8,128)(2,1)}, bf16[4,1024,384]{2,1,0:T(8,128)(2,1)}) custom-call(bf16[256,1024]{1,0:T(8,128)(2,1)S(1)} %get-tuple-element.12.refs_0_, bf16[8,256]{1,0:T(8,128)(2,1)S(1)} %get-tuple-element.13.refs_1_, ...), custom_call_target="tpu_custom_call" | custom-call | tf_op jit(solution)/shard_map/pallas_call | solution.py:738

commit v3 on v2

--- a/solution.py
+++ b/solution.py
@@ -15,7 +15,7 @@
 ANY = pl.BlockSpec(memory_space=pl.ANY)
 HBM = pl.BlockSpec(memory_space=pltpu.HBM)
 TILE = 256
-PIECES = 2
+PIECES = 4
 
 
 def guarded(when, act):
@@ -38,7 +38,7 @@
 
 
 def cut_of(width):
-    return max(width * 5 // 1024, 1) * 128
+    return max(width * 4 // 1024, 1) * 128
 
 
 def fused_kernel(

time: 145 us -> 143 us (0.986)
  Pallas kernels: 143 us -> 141 us
    pallas_call x1, Pallas kernels: 140 us -> 138 us  [fused(): pl.pallas_call(functools.partial(fused_kernel, count, sections, cap, room...]
where the time goes in v3:
time: 143 us; the launch traced here: 141 us
  Pallas kernels  141 us (99%)
    pallas_call x1, Pallas kernels, fused(): pl.pallas_call(functools.partial(fused_kernel, count, sections, cap, room...  138 us
    pallas_call x1, Pallas kernels, publish(): pl.pallas_call(kernel, out_shape=[jax.ShapeDtypeStruct(a.shape, a.dtype)...  3 us

profile of v3, /device:TPU:9, one launch (start us, length us, event | category | flops | bytes accessed | tf_op | source)
XLA Modules:
  0.0 141.5 jit_solution(6497953385887888323)
XLA Ops:
  0.6 137.8 %shard_map.138 = (bf16[256,1024]{1,0:T(8,128)(2,1)S(1)}, bf16[8,256]{1,0:T(8,128)(2,1)S(1)}, bf16[4,1024,384]{2,1,0:T(8,128)(2,1)S(1)}, bf16[4,1024,384]{2,1,0:T(8,128)(2,1)S(1)}) custom-call(bf16[256,1024]{1,0:T(8,128)(2,1)} %bitcast.27, bf16[256,1024]{1,0:T(8,128)(2,1)} %bitcast.28, s32[8,256]{1,0:T(8,128)} %bitcast.29, bf16[8,256]{1,0:T(8,128)(2,1)} %bitcast.30, ...), custom_call_target="tpu_custom_call" | custom-call | tf_op jit(solution)/shard_map/pallas_call | solution.py:638
  138.5 3.0 %shard_map.139 = (bf16[256,1024]{1,0:T(8,128)(2,1)}, bf16[8,256]{1,0:T(8,128)(2,1)}, bf16[4,1024,384]{2,1,0:T(8,128)(2,1)}, bf16[4,1024,384]{2,1,0:T(8,128)(2,1)}) custom-call(bf16[256,1024]{1,0:T(8,128)(2,1)S(1)} %get-tuple-element.12.refs_0_, bf16[8,256]{1,0:T(8,128)(2,1)S(1)} %get-tuple-element.13.refs_1_, ...), custom_call_target="tpu_custom_call" | custom-call | tf_op jit(solution)/shard_map/pallas_call | solution.py:738
